TPU v7x, 32 devices: a whole 2x2x4 slice. The times are simulated.
32 devices in a mesh: seq: 4 (over x, core), vocab: 8 (over z, y).
Axes of the slice: x: 2, y: 2, z: 4, core: 2. Of those that a mesh axis runs over, the one named last changes fastest.
Arguments:
- hidden: bfloat16 [512, 4608], P('seq', 'vocab'), may hold values from -6 to 6
- norm_gain: float32 [4608], replicated, may hold values from -1.5 to 1.5
- unembed: bfloat16 [256000, 4608], P(('seq', 'vocab')), may hold values from -0.375 to 0.375
- targets: int32 [512], P('seq'), may hold values from 0 to 255999
Outputs:
- log_prob: float32 [512], P('seq')
- entropy: float32 [512], P('seq')
All inputs are finite; a program needn't handle non-finite values.
Results may differ from a plain program's by a relative error of at most 0.0012.
Values may be sent and summed in bfloat16 or wider, within the bound.
A program may use at most 128 MiB of HBM per device.

v0:
```python
import jax
import jax.numpy as jnp
from jax import lax
from jax.sharding import PartitionSpec as P

softcap = 30.0
epsilon = 1e-06


def token_stats(logits, target_rows, first):
    capped = softcap * jnp.tanh(logits / softcap)
    weights = jnp.exp(capped - softcap)
    columns = first + lax.broadcasted_iota(jnp.int32, logits.shape, 1)
    chosen = jnp.where(columns == target_rows[:, None], capped, 0.0)
    return jnp.stack(
        [jnp.sum(weights, axis=1), jnp.sum(weights * capped, axis=1), jnp.sum(chosen, axis=1)]
    )


def on_device(hidden, norm_gain, unembed, targets):
    vocab_rows = unembed.shape[0]
    own_tokens = hidden.shape[0]
    first = lax.axis_index(("seq", "vocab")) * vocab_rows
    all_targets = lax.all_gather(targets, "seq", axis=0, tiled=True)
    rows = lax.all_gather(hidden, "vocab", axis=1, tiled=True).astype(jnp.float32)
    scale = lax.rsqrt(jnp.mean(rows * rows, axis=1, keepdims=True) + epsilon)
    normed = (rows * scale * (1.0 + norm_gain)).astype(jnp.bfloat16)
    logits = lax.dot_general(
        lax.all_gather(normed, "seq", axis=0, tiled=True),
        unembed,
        (((1,), (1,)), ((), ())),
        preferred_element_type=jnp.float32,
    )
    stats = token_stats(logits, all_targets, first)
    summed = lax.psum(stats, ("seq", "vocab"))
    mine = lax.dynamic_slice_in_dim(summed, lax.axis_index("seq") * own_tokens, own_tokens, 1)
    total = mine[0]
    moment = mine[1]
    chosen = mine[2]
    log_norm = softcap + jnp.log(total)
    return (chosen - log_norm, log_norm - moment / total)


def solution(mesh):
    return jax.shard_map(
        on_device,
        mesh=mesh,
        in_specs=(P("seq", "vocab"), P(), P(("seq", "vocab"), None), P("seq")),
        out_specs=(P("seq"), P("seq")),
        check_vma=False,
    )
```

profile of v0, /device:TPU:0, one launch (start us, length us, event | category | flops | bytes accessed | tf_op | source)
XLA Modules:
  0.0 194.3 jit_solution(5912990735798231276)
XLA Ops:
  7.2 0.0 all-gather.4.cloned.1.call-start
  7.2 0.7 all-gather.4.cloned.1.call-update
  7.9 0.0 all-gather.6.cloned.1.call-start
  7.9 0.7 broadcast_add_fusion
  8.7 45.4 %all-gather.4.cloned.1.call-done = bf16[128,4608]{0,1:T(8,128)(2,1)} async-done(((bf16[128,576]{0,1:T(8,128)(2,1)}), bf16[128,4608]{0,1:T(8,128)(2,1)}) %all-gather.4.cloned.1.call-update) | async-done | bytes 1179664 | tf_op jit(solution)/shard_map/all_gather | solution.py:25
  54.0 1.9 fusion.1
  55.9 3.9 %fusion.3 = bf16[128,4608]{0,1:T(8,128)(2,1)} fusion(bf16[128,4608]{0,1:T(8,128)(2,1)} %all-gather.4.cloned.1.call-done, f32[4608]{0:T(1024)S(1)} %broadcast_add_fusion, f32[128]{0:T(128)S(1)} %add_rsqrt_fusion), kind=kLoop, calls=%fused_computation.9 | loop fusion | flops 2359296 | bytes 2378240 | tf_op jit(solution)/shard_map/convert_element_type | solution.py:27
  59.8 0.0 all-gather.6.cloned.1.call-update
  59.8 5.2 %all-gather = s32[4,1,128]{2,1,0:T(1,128)S(1)} all-gather(s32[1,1,128]{2,1,0:T(1,128)} %bitcast.15), channel_id=1, replica_groups=mesh['seq'=4,'vocab'=8] {'seq'}, dimensions={0}, use_global_device_ids=true | all-gather | bytes 2560 | tf_op jit(solution)/shard_map/all_gather | solution.py:24
  65.0 31.7 %all-gather.6.cloned.1.call-done = bf16[512,4608]{0,1:T(8,128)(2,1)} async-done(((bf16[128,4608]{0,1:T(8,128)(2,1)}), bf16[512,4608]{0,1:T(8,128)(2,1)}) %all-gather.6.cloned.1.call-update) | async-done | bytes 4718608 | tf_op jit(solution)/shard_map/all_gather | solution.py:29
  96.7 50.8 %fusion = (f32[512]{0:T(512)S(1)}, f32[512]{0:T(512)S(1)}, f32[512]{0:T(512)S(1)}) fusion(s32[512]{0:T(512)S(1)} %bitcast.14, s32[8000]{0:T(1024)S(1)} %iota_add_fusion, bf16[8000,4608]{1,0:T(8,128)(2,1)} %param.6, bf16[512,4608]{0,1:T(8,128)(2,1)} %all-gather.6.cloned.1.call-done), kind=kOutput, calls=%fused_computation.3 | convolution fusion | flops 37785600000 | bytes 78486784 | tf_op jit(solution)/shard_map/dot_general | solution.py:28
  147.6 39.4 %psum.7 = f32[3,512]{1,0:T(4,128)S(1)} all-reduce(f32[3,512]{1,0:T(4,128)S(1)} %pad_maximum_fusion), channel_id=1, replica_groups=mesh['seq'=4,'vocab'=8] {'seq','vocab'}, use_global_device_ids=true, to_apply=%region_4.5 | all-reduce | flops 1536 | bytes 12288 | tf_op jit(solution)/shard_map/psum | solution.py:35
  186.9 0.5 subtract_bitcast_fusion
  (4 shorter events, 0.0 us)
Async XLA Ops:
  7.2 46.9 %all-gather.4.cloned.1.call-start = ((), (), s32[]{:S(2)}) async-start(), calls=%async_computation | async-start | bytes 1327104 | tf_op jit(solution)/shard_map/all_gather | solution.py:25
  7.9 88.8 %all-gather.6.cloned.1.call-start = ((), (), s32[]{:S(2)}) async-start(), calls=%async_computation.1 | async-start | bytes 5898240 | tf_op jit(solution)/shard_map/all_gather | solution.py:29
Sparse Core Ops, SparseCore 0:
  10.2 43.8 all-gather.3
  59.9 36.7 all-gather.5
where the time goes:
time: 195 us; the launch traced here: 194 us
  waiting for transfers between devices  77.7 us (40%)
  matrix products  50.8 us (26%)
  blocking collectives  44.6 us (23%)
  between operations  14.1 us (7%)
  other arithmetic  7.03 us (4%)
    dot_general x1, matrix products, on_device(): lax.dot_general(lax.all_gather(normed, 'seq', axis=0, tiled=True), unembe...  50.8 us
    all_gather x1, waiting for transfers between devices, on_device(): lax.all_gather(hidden, 'vocab', axis=1, tiled=True).astype(jnp.float32)  45.4 us
    psum x1, blocking collectives, on_device(): summed = lax.psum(stats, ('seq', 'vocab'))  39.4 us
    all_gather x1, waiting for transfers between devices, on_device(): lax.all_gather(normed, 'seq', axis=0, tiled=True)  31.7 us
    all_gather x1, blocking collectives, on_device(): all_targets = lax.all_gather(targets, 'seq', axis=0, tiled=True)  5.2 us
  transfers between devices with their start and end apart: 2, of which 2 were waited for; matrix products, arithmetic and copies ran while one was open for 0% of the time, Pallas kernels for 0%

commit v1 on v0

v1 whole, which is shorter than its diff:
```python
import functools

import jax
import jax.numpy as jnp
from jax import lax
from jax.experimental import pallas as pl
from jax.experimental.pallas import tpu as pltpu
from jax.sharding import PartitionSpec as P

softcap = 30.0
epsilon = 1e-06
CORES = 2
QUARTERS = 4
MESH = pl.DeviceIdType.MESH
ORDERS = (("x", "y", "z"), ("y", "x", "z"), ("z", "x", "y"), ("z", "y", "x"))


def gather_kernel(sizes, hidden_ref, gain_ref, targets_ref, normed_ref, all_targets_ref,
                  held, load_sem, send_sem, recv_sem, pair_send, pair_recv, id_send, id_recv):
    X, Y, Z = sizes["x"], sizes["y"], sizes["z"]
    seq, vocab = lax.axis_index("seq"), lax.axis_index("vocab")
    core = lax.rem(seq, CORES)
    me = {"x": seq // CORES, "y": lax.rem(vocab, Y), "z": vocab // Y}
    rows, part = held.shape[5], held.shape[6]

    def device(**moved):
        at = {**me, **moved}
        return {"seq": at["x"] * CORES + at.get("core", core), "vocab": at["z"] * Y + at["y"]}

    loads = [
        pltpu.make_async_copy(
            hidden_ref.at[pl.ds(q * rows, rows)],
            held.at[core, q, me["z"], me["y"], me["x"]],
            load_sem.at[q],
        )
        for q in range(QUARTERS)
    ]
    for load in loads:
        load.start()

    seqs = X * CORES
    greeted = [{"seq": lax.rem(seq + k, seqs), "vocab": vocab} for k in range(1, seqs)]
    for d in ("y", "z"):
        n = sizes[d]
        for k in sorted({1, n - 1}) if n > 1 else ():
            greeted.append(device(**{d: lax.rem(me[d] + k, n)}))
    barrier = pltpu.get_barrier_semaphore()
    for other in greeted:
        pl.semaphore_signal(barrier, inc=1, device_id=other, device_id_type=MESH)
    all_targets_ref[seq] = targets_ref[...]
    for load in loads:
        load.wait()
    pl.semaphore_wait(barrier, len(greeted))

    sends = []

    def targets_copy(k, to, slot):
        return pltpu.make_async_remote_copy(
            src_ref=targets_ref, dst_ref=all_targets_ref.at[slot],
            send_sem=id_send.at[k - 1], recv_sem=id_recv.at[k - 1],
            device_id={"seq": to, "vocab": vocab}, device_id_type=MESH,
        )

    def quarter(q):
        done = set()
        for axis, d in enumerate(ORDERS[q]):
            n = sizes[d]
            ahead = n // 2 if q % 2 == 0 else (n - 1) // 2
            behind = n - 1 - ahead

            def region(i):
                index = tuple(
                    i if e == d else (pl.ds(0, sizes[e]) if e in done else me[e]) for e in ("z", "y", "x")
                )
                return held.at[(core, q) + index]

            def copy(step, way):
                i = lax.rem(me[d] + (n - step + 1 if way == 0 else step - 1), n)
                sem = (q, axis, way, step - 1)
                return pltpu.make_async_remote_copy(
                    src_ref=region(i), dst_ref=region(i),
                    send_sem=send_sem.at[sem], recv_sem=recv_sem.at[sem],
                    device_id=device(**{d: lax.rem(me[d] + (1 if way == 0 else n - 1), n)}),
                    device_id_type=MESH,
                )

            for step in range(1, max(ahead, behind) + 1):
                going = [copy(step, w) for w, last in ((0, ahead), (1, behind)) if step <= last]
                for c in going:
                    c.start()
                sends.extend(going)
                yield
                for c in going:
                    c.wait_recv()
            done.add(d)
        pair = pltpu.make_async_remote_copy(
            src_ref=held.at[core, q], dst_ref=held.at[core, q],
            send_sem=pair_send.at[q], recv_sem=pair_recv.at[q],
            device_id=device(core=1 - core), device_id_type=MESH,
        )
        pair.start()
        sends.append(pair)
        pairs[q] = pair

    pairs = {}
    running = [quarter(q) for q in range(QUARTERS)]
    first = True
    while running:
        running = [g for g in running if next(g, "end") is None]
        if first:
            ids = [targets_copy(k, lax.rem(seq + k, seqs), seq) for k in range(1, seqs)]
            for c in ids:
                c.start()
            first = False
    for c in ids:
        c.wait()

    width = Z * Y * part
    for q in range(QUARTERS):
        pairs[q].wait_recv()

        def block(i, _, q=q):
            c, x = lax.rem(i, CORES), i // CORES
            squares = jnp.zeros((rows, 1), jnp.float32)
            for v in range(Z * Y):
                values = held[c, q, v // Y, v % Y, x].astype(jnp.float32)
                squares += jnp.sum(values * values, axis=1, keepdims=True)
            scale = lax.rsqrt(squares / width + epsilon)
            start = pl.multiple_of((x * CORES + c) * (rows * QUARTERS) + q * rows, rows)
            for v in range(Z * Y):
                values = held[c, q, v // Y, v % Y, x].astype(jnp.float32)
                normed_ref[pl.ds(start, rows), v * part:(v + 1) * part] = (
                    values * scale * (1.0 + gain_ref[v])
                ).astype(jnp.bfloat16)
            return 0

        lax.fori_loop(0, X * CORES, block, 0)
    for c in sends:
        c.wait_send()


def exchange_kernel(seqs, vocabs, stats_ref, log_prob_ref, entropy_ref, arrived, send_sem, recv_sem):
    count = seqs * vocabs
    seq, vocab = lax.axis_index("seq"), lax.axis_index("vocab")
    me = seq * vocabs + vocab

    def place(k):
        other = lax.rem(me + k, count)
        return other, {"seq": other // vocabs, "vocab": lax.rem(other, vocabs)}

    barrier = pltpu.get_barrier_semaphore()

    def greet(k, _):
        pl.semaphore_signal(barrier, inc=1, device_id=place(k)[1], device_id_type=MESH)
        return 0

    lax.fori_loop(1, count, greet, 0)
    arrived[me] = stats_ref[seq]
    pl.semaphore_wait(barrier, count - 1)

    def copy(k, slot):
        other, where = place(k)
        return pltpu.make_async_remote_copy(
            src_ref=stats_ref.at[other // vocabs], dst_ref=arrived.at[slot],
            send_sem=send_sem.at[k], recv_sem=recv_sem.at[slot],
            device_id=where, device_id_type=MESH,
        )

    def send(k, _):
        copy(k, me).start()
        return 0

    def sent(k, _):
        copy(k, me).wait_send()
        return 0

    def receive(k, _):
        copy(k, place(k)[0]).wait_recv()
        return 0

    lax.fori_loop(1, count, send, 0)
    lax.fori_loop(1, count, receive, 0)
    sums = arrived[0]
    for i in range(1, count):
        sums = sums + arrived[i]
    total, moment, chosen = sums[0:1], sums[1:2], sums[2:3]
    log_norm = softcap + jnp.log(total)
    log_prob_ref[...] = chosen - log_norm
    entropy_ref[...] = log_norm - moment / total
    lax.fori_loop(1, count, sent, 0)


def token_stats(logits, target_rows, first):
    capped = softcap * jnp.tanh(logits / softcap)
    weights = jnp.exp(capped - softcap)
    columns = first + lax.broadcasted_iota(jnp.int32, logits.shape, 1)
    chosen = jnp.where(columns == target_rows[:, None], capped, 0.0)
    return jnp.stack(
        [jnp.sum(weights, axis=1), jnp.sum(weights * capped, axis=1), jnp.sum(chosen, axis=1)]
    )


def on_device(seqs, vocabs, hidden, norm_gain, unembed, targets):
    vocab_rows, width = unembed.shape
    own, part = hidden.shape
    first = lax.axis_index(("seq", "vocab")) * vocab_rows
    Y = 2 ** ((vocabs.bit_length() - 1) // 2)
    sizes = {"x": seqs // CORES, "y": Y, "z": vocabs // Y}
    steps = max(max(n // 2 for n in sizes.values()), 1)
    vmem = pl.BlockSpec(memory_space=pltpu.VMEM)
    normed, all_targets = pl.pallas_call(
        functools.partial(gather_kernel, sizes),
        out_shape=(
            jax.ShapeDtypeStruct((seqs * own, width), jnp.bfloat16),
            jax.ShapeDtypeStruct((seqs, 1, own), jnp.int32),
        ),
        in_specs=[pl.BlockSpec(memory_space=pltpu.HBM), vmem, vmem],
        out_specs=(vmem, vmem),
        scratch_shapes=[
            pltpu.VMEM((CORES, QUARTERS, sizes["z"], Y, sizes["x"], own // QUARTERS, part), jnp.bfloat16),
            pltpu.SemaphoreType.DMA((QUARTERS,)),
            pltpu.SemaphoreType.DMA((QUARTERS, 3, 2, steps)),
            pltpu.SemaphoreType.DMA((QUARTERS, 3, 2, steps)),
            pltpu.SemaphoreType.DMA((QUARTERS,)),
            pltpu.SemaphoreType.DMA((QUARTERS,)),
            pltpu.SemaphoreType.DMA((seqs - 1,)),
            pltpu.SemaphoreType.DMA((seqs - 1,)),
        ],
        compiler_params=pltpu.CompilerParams(collective_id=0, has_side_effects=True),
        name="gather_norm",
    )(hidden, norm_gain.reshape(vocabs, 1, part), targets.reshape(1, own))
    logits = lax.dot_general(
        normed, unembed, (((1,), (1,)), ((), ())), preferred_element_type=jnp.float32
    )
    stats = token_stats(logits, all_targets.reshape(seqs * own), first)
    stats = jnp.transpose(stats.reshape(3, seqs, own), (1, 0, 2))
    log_prob, entropy = pl.pallas_call(
        functools.partial(exchange_kernel, seqs, vocabs),
        out_shape=(jax.ShapeDtypeStruct((1, own), jnp.float32),) * 2,
        in_specs=[vmem],
        out_specs=(vmem, vmem),
        scratch_shapes=[
            pltpu.VMEM((seqs * vocabs, 3, own), jnp.float32),
            pltpu.SemaphoreType.DMA((seqs * vocabs,)),
            pltpu.SemaphoreType.DMA((seqs * vocabs,)),
        ],
        compiler_params=pltpu.CompilerParams(collective_id=1, has_side_effects=True),
        name="exchange",
    )(stats)
    return log_prob.reshape(own), entropy.reshape(own)


def solution(mesh):
    return jax.shard_map(
        functools.partial(on_device, mesh.shape["seq"], mesh.shape["vocab"]),
        mesh=mesh,
        in_specs=(P("seq", "vocab"), P(), P(("seq", "vocab"), None), P("seq")),
        out_specs=(P("seq"), P("seq")),
        check_vma=False,
    )
```

time: 195 us -> 110 us (0.56)
  waiting for transfers between devices: 77.7 us -> 0 us
  Pallas kernels: 0 us -> 53.1 us
  blocking collectives: 44.6 us -> 0 us
  between operations: 14.1 us -> 0.67 us
  other arithmetic: 7.03 us -> 0.61 us
  local copies, waits for them, and re-layouts: 0.01 us -> 5.37 us
    all_gather x2 -> x0, waiting for transfers between devices: 77 us -> none  [the longest x1 45.4 us: on_device(): lax.all_gather(hidden, 'vocab', axis=1, tiled=True).astype(jnp.float32)]
    pallas_call x0 -> x2, Pallas kernels: none -> 53.1 us  [the longest x1 42.3 us: on_device(): pl.pallas_call(functools.partial(gather_kernel, sizes), out_shape=(jax.Sh...]
    psum x1 -> x0, blocking collectives: 39.4 us -> none  [on_device(): summed = lax.psum(stats, ('seq', 'vocab'))]
    all_gather x1 -> x0, blocking collectives: 5.2 us -> none  [on_device(): all_targets = lax.all_gather(targets, 'seq', axis=0, tiled=True)]
    unnamed x0 -> x3, local copies, waits for them, and re-layouts: none -> 3.96 us
    convert_element_type x1 -> x0, other arithmetic: 3.85 us -> none  [on_device(): normed = (rows * scale * (1.0 + norm_gain)).astype(jnp.bfloat16)]
  transfers between devices with their start and end apart: 2 -> 0, of which waited for: 2 -> 0; matrix products, arithmetic and copies ran while one was open for 0% -> 0% of each run, Pallas kernels for 0% -> 0%
where the time goes in v1:
time: 110 us
  Pallas kernels  53.1 us (48%)
  matrix products  50.2 us (46%)
  local copies, waits for them, and re-layouts  5.37 us (5%)
    dot_general x1, matrix products, on_device(): lax.dot_general(normed, unembed, (((1,), (1,)), ((), ())), preferred_elem...  50.2 us
    pallas_call x1, Pallas kernels, on_device(): pl.pallas_call(functools.partial(gather_kernel, sizes), out_shape=(jax.Sh...  42.3 us
    pallas_call x1, Pallas kernels, on_device(): pl.pallas_call(functools.partial(exchange_kernel, seqs, vocabs), out_shap...  10.8 us
    unnamed x3, local copies, waits for them, and re-layouts  3.96 us

profile of v1, /device:TPU:0, one launch (start us, length us, event | category | flops | bytes accessed | tf_op | source)
XLA Modules:
  0.0 110.0 jit_solution(2198318634981307641)
XLA Ops:
  0.6 1.7 %copy.6.hidden_ref = bf16[128,576]{1,0:T(8,128)(2,1)} copy(bf16[128,576]{0,1:T(8,128)(2,1)} %param.4) | data formatting | bytes 294912 | tf_op args[0]
  2.3 1.4 %reshape.24.gain_ref = f32[8,1,576]{2,1,0:T(1,128)} reshape(f32[4608]{0:T(1024)} %param.5) | data formatting | bytes 36864 | tf_op jit(solution)/shard_map/reshape | solution.py:231
  3.8 42.3 %gather_norm.1 = (bf16[512,4608]{1,0:T(8,128)(2,1)}, s32[4,1,128]{2,1,0:T(1,128)}) custom-call(bf16[128,576]{1,0:T(8,128)(2,1)} %copy.6.hidden_ref, f32[8,1,576]{2,1,0:T(1,128)} %reshape.24.gain_ref, s32[1,128]{1,0:T(1,128)} %bitcast.14), custom_call_target="tpu_custom_call" | custom-call | tf_op jit(solution)/shard_map/gather_norm/pallas_call | solution.py:211
  46.1 50.2 %fusion = (f32[512]{0:T(512)S(1)}, f32[512]{0:T(512)S(1)}, f32[512]{0:T(512)S(1)}) fusion(s32[512]{0:T(512)} %bitcast.15, s32[8000]{0:T(1024)S(1)} %iota_add_fusion, bf16[512,4608]{1,0:T(8,128)(2,1)} %get-tuple-element.6, bf16[8000,4608]{1,0:T(8,128)(2,1)} %param.6), kind=kOutput, calls=%fused_computation.3 | convolution fusion | flops 37785600000 | bytes 78486784 | tf_op jit(solution)/shard_map/dot_general | solution.py:232
  96.3 0.6 maximum_bitcast_fusion.stats_ref
  96.9 10.8 %exchange.1 = (f32[1,128]{1,0:T(1,128)}, f32[1,128]{1,0:T(1,128)}) custom-call(f32[4,3,128]{2,1,0:T(4,128)} %maximum_bitcast_fusion.stats_ref), custom_call_target="tpu_custom_call" | custom-call | tf_op jit(solution)/shard_map/exchange/pallas_call | solution.py:237
  107.7 1.1 %copy.9 = f32[128]{0:T(128)} copy(f32[128]{0:T(128)} %bitcast.17) | data formatting | bytes 1024
  108.8 1.1 %copy.10 = f32[128]{0:T(128)} copy(f32[128]{0:T(128)} %bitcast.16) | data formatting | bytes 1024
  (1 shorter events, 0.0 us)
